TPU v7x, 32 devices: a whole 2x2x4 slice. The times are simulated.
32 devices in a mesh: dp: 2 (over y), fsdp: 16 (over z, x, core).
Axes of the slice: x: 2, y: 2, z: 4, core: 2. Of those that a mesh axis runs over, the one named last changes fastest.
Arguments:
- queries: bfloat16 [6144, 2560], P(('dp', 'fsdp')), may hold values from -8 to 8
- keys: bfloat16 [6144, 2560], P(('dp', 'fsdp')), may hold values from -8 to 8
- values: bfloat16 [6144, 2560], P(('dp', 'fsdp')), may hold values from -6 to 6
- lengths: int32 [16, 2, 4], P('fsdp'), may hold values from 0 to 192, as said below
- normalized_weight: bfloat16 [2560, 5120], P(None, 'fsdp'), may hold values from -1 to 1
- block_scale_codes: int32 [40, 5120], P(None, 'fsdp'), may hold values from 0 to 255
- scale_group_factor: float32 [5, 5120], P(None, 'fsdp'), may hold values from 0.01 to 0.03
- scale_group_offset: float32 [5, 5120], P(None, 'fsdp'), may hold values from 0.005 to 0.015
- adapter_down_weight: bfloat16 [64, 2560], P(None, 'fsdp'), may hold values from -0.125 to 0.125
- adapter_up_weight: bfloat16 [64, 5120], P(None, 'fsdp'), may hold values from -0.75 to 0.75
- cotangent: bfloat16 [6144, 5120], P(('dp', 'fsdp')), may hold values from -6 to 6
Outputs:
- projection_output: bfloat16 [6144, 5120], P(('dp', 'fsdp'))
- attention_gradient: bfloat16 [6144, 2560], P(('dp', 'fsdp'))
- down_grad: float32 [64, 2560], P(None, 'fsdp')
- adapter_up_gradient: float32 [64, 5120], P(None, 'fsdp')
Inputs may be any that keep to these rules, and one draw needn't show every extreme that they name: The 4 lengths of each block sum to 192; zero lengths, if any, come last; some block is a single document of 192 tokens.
All inputs are finite; a program needn't handle non-finite values.
Results may differ from a plain program's by a relative error of at most 0.0059.
Values may be sent and summed in bfloat16 or wider, within the bound.
A program may use at most 192 MiB of HBM per device.

v0:
```python
import jax
import jax.numpy as jnp
from jax import lax
from jax.sharding import PartitionSpec as P

HEAD_SIZE = 128
QBLOCK = 64
SCALE_GROUP = 8


adapter_scale = 0.25


def dequantize(normalized_weight, block_scale_codes, scale_group_factor, scale_group_offset):
    spread_scale = jnp.repeat(scale_group_factor, SCALE_GROUP, axis=0)
    spread_offset = jnp.repeat(scale_group_offset, SCALE_GROUP, axis=0)
    absmax = spread_scale * (block_scale_codes.astype(jnp.float32) + 1.0) / 256.0 + spread_offset
    return (normalized_weight.astype(jnp.float32) * jnp.repeat(absmax, QBLOCK, axis=0)).astype(
        jnp.bfloat16
    )


def attend(queries, keys, values, doc_lengths):
    tokens = queries.shape[0]
    head_count = queries.shape[1] // HEAD_SIZE
    query_heads = queries.reshape(tokens, head_count, HEAD_SIZE)
    key_heads = keys.reshape(tokens, head_count, HEAD_SIZE)
    value_heads = values.reshape(tokens, head_count, HEAD_SIZE)
    doc_ends = jnp.cumsum(doc_lengths)
    places = jnp.arange(tokens, dtype=jnp.int32)
    segment = jnp.sum((doc_ends[None, :] <= places[:, None]).astype(jnp.int32), axis=1)
    allowed = (segment[:, None] == segment[None, :]) & (places[None, :] <= places[:, None])
    scores = jnp.einsum(
        "qhe,khe->hqk", query_heads, key_heads, preferred_element_type=jnp.float32
    ) * HEAD_SIZE ** (-0.5)
    scores = jnp.where(allowed[None], scores, -jnp.inf)
    row_max = jnp.max(scores, axis=-1, keepdims=True)
    weights = jnp.exp(scores - row_max)
    total = jnp.sum(weights, axis=-1)
    summed = jnp.einsum(
        "hqk,khe->qhe",
        weights.astype(jnp.bfloat16),
        value_heads,
        preferred_element_type=jnp.float32,
    )
    return (
        (summed / jnp.transpose(total)[:, :, None])
        .astype(jnp.bfloat16)
        .reshape(tokens, head_count * HEAD_SIZE)
    )


def apply_columns(attention_output, grad_view, column_piece):
    block_product = jnp.einsum(
        "ti,iabs->tabs", attention_output, column_piece, preferred_element_type=jnp.float32
    )
    backward = jnp.einsum(
        "tabs,iabs->ti", grad_view, column_piece, preferred_element_type=jnp.float32
    )
    return (block_product, backward)


def per_device(
    queries,
    keys,
    values,
    lengths,
    normalized_weight,
    block_scale_codes,
    scale_group_factor,
    scale_group_offset,
    adapter_down_weight,
    adapter_up_weight,
    cotangent,
):
    tokens = queries.shape[0]
    row_index = lax.axis_index("dp")
    own_lengths = lax.dynamic_index_in_dim(lengths[0], row_index, 0, keepdims=False)
    attention_output = attend(queries, keys, values, own_lengths)
    down_full, complete_up_gradient = (
        lax.all_gather(adapter_down_weight, "fsdp", axis=1, tiled=True),
        lax.all_gather(adapter_up_weight, "fsdp", axis=1, tiled=True),
    )
    fsdp_size = lax.axis_size("fsdp")
    row_size = lax.axis_size("dp")
    local_base = dequantize(
        normalized_weight, block_scale_codes, scale_group_factor, scale_group_offset
    )
    feature_count = local_base.shape[0]
    part_width = local_base.shape[1] // row_size
    base_view = local_base.reshape(feature_count, 1, row_size, part_width)
    grad_view = cotangent.reshape(tokens, fsdp_size, row_size, part_width)
    product, backward = apply_columns(
        attention_output, grad_view, lax.all_gather(base_view, "fsdp", axis=1, tiled=True)
    )
    reduced_activation = jnp.dot(
        attention_output, down_full.T, preferred_element_type=jnp.float32
    ).astype(jnp.bfloat16)
    projection_output = (
        product.reshape(tokens, -1)
        + adapter_scale
        * jnp.dot(reduced_activation, complete_up_gradient, preferred_element_type=jnp.float32)
    ).astype(jnp.bfloat16)
    reduced_gradient = (
        adapter_scale
        * jnp.dot(cotangent, complete_up_gradient.T, preferred_element_type=jnp.float32)
    ).astype(jnp.bfloat16)
    attention_gradient = (
        backward + jnp.dot(reduced_gradient, down_full, preferred_element_type=jnp.float32)
    ).astype(jnp.bfloat16)
    down_part = jnp.dot(reduced_gradient.T, attention_output, preferred_element_type=jnp.float32)
    partial_up_gradient = adapter_scale * jnp.dot(
        reduced_activation.T, cotangent, preferred_element_type=jnp.float32
    )
    down_share, up_share = (
        lax.psum_scatter(down_part, "fsdp", scatter_dimension=1, tiled=True),
        lax.psum_scatter(partial_up_gradient, "fsdp", scatter_dimension=1, tiled=True),
    )
    down_grad, adapter_up_gradient = lax.psum((down_share, up_share), "dp")
    return (projection_output, attention_gradient, down_grad, adapter_up_gradient)


def solution(mesh):
    return jax.shard_map(
        per_device,
        mesh=mesh,
        in_specs=(
            P(("dp", "fsdp"), None),
            P(("dp", "fsdp"), None),
            P(("dp", "fsdp"), None),
            P("fsdp", None, None),
            P(None, "fsdp"),
            P(None, "fsdp"),
            P(None, "fsdp"),
            P(None, "fsdp"),
            P(None, "fsdp"),
            P(None, "fsdp"),
            P(("dp", "fsdp"), None),
        ),
        out_specs=(
            P(("dp", "fsdp"), None),
            P(("dp", "fsdp"), None),
            P(None, "fsdp"),
            P(None, "fsdp"),
        ),
        check_vma=False,
    )
```

profile of v0, /device:TPU:11, one launch (start us, length us, event | category | flops | bytes accessed | tf_op | source)
XLA Modules:
  0.0 342.7 jit_solution(10687420981906688608)
XLA Ops:
  8.5 18.1 %all-gather.1 = bf16[16,320,64]{1,2,0:T(8,128)(2,1)S(1)} all-gather(bf16[1,320,64]{1,2,0:T(8,128)(2,1)} %bitcast.100), channel_id=1, replica_groups=mesh['dp'=2,'fsdp'=16] {'fsdp'}, dimensions={0}, use_global_device_ids=true | all-gather | bytes 696320 | tf_op jit(solution)/shard_map/all_gather | solution.py:82
  27.9 2.4 reshape.120
  30.3 1.8 fusion.13
  32.2 2.1 fusion.3
  35.1 1.8 fusion.25
  36.9 1.8 convolution_bitcast_fusion.1
  38.8 22.9 %all-gather = bf16[16,160,64]{1,2,0:T(8,128)(2,1)S(1)} all-gather(bf16[1,160,64]{1,2,0:T(8,128)(2,1)S(1)} %bitcast.101), channel_id=1, replica_groups=mesh['dp'=2,'fsdp'=16] {'fsdp'}, dimensions={0}, use_global_device_ids=true | all-gather | bytes 348160 | tf_op jit(solution)/shard_map/all_gather | solution.py:81
  62.8 1.6 convolution_convert_fusion
  64.4 1.5 convolution_multiply_fusion.1
  66.0 3.0 copy.74
  69.1 2.1 broadcast_in_dim.34
  71.2 5.3 %copy.66 = f32[2560,320]{0,1:T(8,128)} copy(f32[2560,320]{1,0:T(8,128)} %bitcast.94) | data formatting | bytes 6553600 | tf_op jit(solution)/shard_map/reshape | solution.py:18
  76.5 4.0 %multiply_convert_fusion = bf16[2560,320]{0,1:T(8,128)(2,1)} fusion(f32[2560,320]{0,1:T(8,128)} %copy.66, bf16[2560,320]{0,1:T(8,128)(2,1)} %param.15), kind=kLoop, calls=%fused_computation.11 | loop fusion | flops 2457600 | bytes 6553600 | tf_op jit(solution)/shard_map/convert_element_type | solution.py:18
  80.6 2.5 copy.69
  83.2 15.5 %reduce-scatter.7.cloned.1.call-done = f32[160,64]{1,0:T(8,128)} async-done(((f32[2560,64]{1,0:T(8,128)}), f32[160,64]{1,0:T(8,128)}) %reduce-scatter.7.cloned.1.call-update) | async-done | bytes 40976
  99.6 7.0 %psum.14 = f32[64,160]{1,0:T(8,128)} all-reduce(f32[64,160]{1,0:T(8,128)S(1)} %copy.73), channel_id=1, replica_groups=mesh['dp'=2,'fsdp'=16] {'dp'}, use_global_device_ids=true, to_apply=%region_5.6 | all-reduce | flops 10240 | bytes 81920 | tf_op jit(solution)/shard_map/psum | solution.py:119
  106.6 58.9 %reduce-scatter.9.cloned.1.call-done = f32[320,64]{1,0:T(8,128)} async-done(((f32[5120,64]{1,0:T(8,128)}), f32[320,64]{1,0:T(8,128)}) %reduce-scatter.9.cloned.1.call-update) | async-done | bytes 81936
  165.5 1.7 copy.75
  167.2 135.4 %all-gather.4.cloned.1.call-done = bf16[2560,16,2,160]{0,3,2,1:T(8,128)(2,1)} async-done(((bf16[2560,1,2,160]{0,3,2,1:T(8,128)(2,1)}), bf16[2560,16,2,160]{0,3,2,1:T(8,128)(2,1)}) %all-gather.4.cloned.1.call-update) | async-done | bytes 26214416 | tf_op jit(solution)/shard_map/all_gather | solution.py:94
  302.6 15.1 %fusion.16 = f32[192,5120]{1,0:T(8,128)} fusion(bf16[5120,2560]{1,0:T(8,128)(2,1)} %bitcast.103, bf16[20,24,8,128]{3,2,1,0:T(8,128)(2,1)} %copy-done.5), kind=kOutput, calls=%fused_computation.26 | convolution fusion | flops 5033164800 | bytes 31129600 | tf_op jit(solution)/shard_map/ti,iabs->tabs/dot_general | solution.py:54
  317.6 4.2 %fusion.1 = bf16[192,5120]{1,0:T(8,128)(2,1)} fusion(f32[192,5120]{1,0:T(8,128)} %fusion.16, bf16[192,64]{0,1:T(8,128)(2,1)S(1)} %convolution_convert_fusion, bf16[5120,64]{0,1:T(8,128)(2,1)S(1)} %copy-done.3), kind=kOutput, calls=%fused_computation.2 | convolution fusion | flops 128778240 | bytes 6578176 | tf_op jit(solution)/shard_map/dot_general | solution.py:102
  321.9 11.4 %convolution_bitcast_fusion = f32[192,2560]{1,0:T(8,128)S(1)} fusion(bf16[2560,16,2,160]{0,3,2,1:T(8,128)(2,1)} %all-gather.4.cloned.1.call-done, bf16[192,16,2,160]{0,3,2,1:T(8,128)(2,1)S(1)} %bitcast.97), kind=kOutput, calls=%fused_computation.7 | convolution fusion | flops 5033164800 | bytes 30146560 | tf_op jit(solution)/shard_map/tabs,iabs->ti/dot_general | solution.py:57
  333.3 1.4 fusion.2
  334.7 1.5 copy.111
  (41 shorter events, 5.7 us)
Async XLA Ops:
  7.2 25.0 %copy-start = (bf16[192,2560]{1,0:T(8,128)(2,1)S(1)}, bf16[192,2560]{1,0:T(8,128)(2,1)}, u32[]{:S(2)}) copy-start(bf16[192,2560]{1,0:T(8,128)(2,1)} %param.12) | copy-start | bytes 2949124
  7.2 23.1 %copy-start.2 = (bf16[192,5120]{1,0:T(8,128)(2,1)S(1)}, bf16[192,5120]{1,0:T(8,128)(2,1)}, u32[]{:S(2)}) copy-start(bf16[192,5120]{1,0:T(8,128)(2,1)} %param.21) | copy-start | bytes 5898244
  7.2 91.5 %reduce-scatter.7.cloned.1.call-start = ((), (), s32[]{:S(2)}) async-start(), calls=%async_computation.4 | async-start | bytes 1392640
  32.1 3.0 copy-start.10
  35.1 3.7 %copy-start.7 = (bf16[64,160]{1,0:T(8,128)(2,1)S(1)}, bf16[64,160]{1,0:T(8,128)(2,1)}, u32[]{:S(2)}) copy-start(bf16[64,160]{1,0:T(8,128)(2,1)} %param.19) | copy-start | bytes 61444
  36.9 1.9 copy-start.5
  38.7 126.8 %reduce-scatter.9.cloned.1.call-start = ((), (), s32[]{:S(2)}) async-start(), calls=%async_computation.5 | async-start | bytes 2785280
  65.9 3.1 copy-start.6
  66.0 3.1 copy-start.8
  66.0 3.1 copy-start.9
  69.0 233.6 %all-gather.4.cloned.1.call-start = ((), (), s32[]{:S(2)}) async-start(), calls=%async_computation.2 | async-start | bytes 27852800 | tf_op jit(solution)/shard_map/all_gather | solution.py:94
  80.6 254.1 %all-reduce.2.cloned.1.call-start = ((), (), s32[]{:S(2)}) async-start(), calls=%async_computation.3 | async-start | bytes 196608 | tf_op jit(solution)/shard_map/psum | solution.py:119
  302.6 15.1 %copy-start.3 = (bf16[5120,64]{0,1:T(8,128)(2,1)S(1)}, bf16[5120,64]{0,1:T(8,128)(2,1)}, u32[]{:S(2)}) copy-start(bf16[5120,64]{0,1:T(8,128)(2,1)} %reshape.120) | copy-start | bytes 1966084
  317.6 4.2 %copy-start.4 = (bf16[192,5120]{0,1:T(8,128)(2,1)S(1)}, bf16[192,5120]{0,1:T(8,128)(2,1)}, u32[]{:S(2)}) copy-start(bf16[192,5120]{0,1:T(8,128)(2,1)} %copy.69) | copy-start | bytes 5898244
  321.9 14.3 %copy-start.1 = (bf16[192,2560]{1,0:T(8,128)(2,1)S(1)}, bf16[192,2560]{1,0:T(8,128)(2,1)}, u32[]{:S(2)}) copy-start(bf16[192,2560]{1,0:T(8,128)(2,1)} %param.12) | copy-start | bytes 2949124
Sparse Core Ops, SparseCore 0:
  38.9 59.7 reduce-scatter.6
  102.4 63.0 reduce-scatter.8
  167.7 134.8 all-gather.3
  305.2 20.5 all-reduce.1
where the time goes:
time: 345 us; the launch traced here: 343 us
  waiting for transfers between devices  210 us (61%)
  blocking collectives  48 us (14%)
  matrix products  42.7 us (12%)
  local copies, waits for them, and re-layouts  22.8 us (7%)
  between operations  13.9 us (4%)
  other arithmetic  5.3 us (2%)
    all_gather x1, waiting for transfers between devices, per_device(): lax.all_gather(base_view, 'fsdp', axis=1, tiled=True)  135 us
    unnamed x6, waiting for transfers between devices  74.5 us
    all_gather x1, blocking collectives, per_device(): lax.all_gather(adapter_down_weight, 'fsdp', axis=1, tiled=True)  22.9 us
    all_gather x1, blocking collectives, per_device(): lax.all_gather(adapter_up_weight, 'fsdp', axis=1, tiled=True)  18.1 us
    dot_general x1, matrix products, apply_columns(): jnp.einsum('ti,iabs->tabs', attention_output, column_piece, preferred_ele...  15.1 us
    unnamed x29, local copies, waits for them, and re-layouts  12.9 us
    dot_general x1, matrix products, apply_columns(): jnp.einsum('tabs,iabs->ti', grad_view, column_piece, preferred_element_ty...  11.4 us
    psum x1, blocking collectives, per_device(): down_grad, adapter_up_gradient = lax.psum((down_share, up_share), 'dp')  6.98 us
  transfers between devices with their start and end apart: 4, of which 3 were waited for; matrix products, arithmetic and copies ran while one was open for 16% of the time, Pallas kernels for 0%

commit v1 on v0

v1 whole, which is shorter than its diff:
```python
import functools

import jax
import jax.numpy as jnp
from jax import lax
from jax.experimental import pallas as pl
from jax.experimental.pallas import tpu as pltpu
from jax.sharding import PartitionSpec as P

HEAD_SIZE = 128
QBLOCK = 64
SCALE_GROUP = 8


adapter_scale = 0.25


def dequantize(normalized_weight, block_scale_codes, scale_group_factor, scale_group_offset):
    spread_scale = jnp.repeat(scale_group_factor, SCALE_GROUP, axis=0)
    spread_offset = jnp.repeat(scale_group_offset, SCALE_GROUP, axis=0)
    absmax = spread_scale * (block_scale_codes.astype(jnp.float32) + 1.0) / 256.0 + spread_offset
    return (normalized_weight.astype(jnp.float32) * jnp.repeat(absmax, QBLOCK, axis=0)).astype(
        jnp.bfloat16
    )


def attend(queries, keys, values, doc_lengths):
    tokens = queries.shape[0]
    head_count = queries.shape[1] // HEAD_SIZE
    query_heads = queries.reshape(tokens, head_count, HEAD_SIZE)
    key_heads = keys.reshape(tokens, head_count, HEAD_SIZE)
    value_heads = values.reshape(tokens, head_count, HEAD_SIZE)
    doc_ends = jnp.cumsum(doc_lengths)
    places = jnp.arange(tokens, dtype=jnp.int32)
    segment = jnp.sum((doc_ends[None, :] <= places[:, None]).astype(jnp.int32), axis=1)
    allowed = (segment[:, None] == segment[None, :]) & (places[None, :] <= places[:, None])
    scores = jnp.einsum(
        "qhe,khe->hqk", query_heads, key_heads, preferred_element_type=jnp.float32
    ) * HEAD_SIZE ** (-0.5)
    scores = jnp.where(allowed[None], scores, -jnp.inf)
    row_max = jnp.max(scores, axis=-1, keepdims=True)
    weights = jnp.exp(scores - row_max)
    total = jnp.sum(weights, axis=-1)
    summed = jnp.einsum(
        "hqk,khe->qhe",
        weights.astype(jnp.bfloat16),
        value_heads,
        preferred_element_type=jnp.float32,
    )
    return (
        (summed / jnp.transpose(total)[:, :, None])
        .astype(jnp.bfloat16)
        .reshape(tokens, head_count * HEAD_SIZE)
    )


MESH = pl.DeviceIdType.MESH


def ring_kernel(scatter, third, *refs):
    if scatter:
        block, parts, out, mine, sems, ring_send, ring_recv, row_send, row_recv = refs[:9]
        core_send, core_recv, part_send, part_recv = refs[9:]
    else:
        block, out, sems, ring_send, ring_recv, row_send, row_recv, core_send, core_recv = refs
    n = lax.axis_size("fsdp")
    chips = n // 2
    half = chips // 2
    row = lax.axis_index("dp")
    me = lax.axis_index("fsdp")
    chip, core = me // 2, me % 2
    place = jnp.where(chip % 2 == 0, chip // 2, chips - 1 - chip // 2)

    def device_at(where):
        where = (where + chips) % chips
        there = jnp.where(where < half, 2 * where, 2 * (chips - 1 - where) + 1)
        return 2 * there + core

    neighbour = (device_at(place + 1), device_at(place - 1))
    twin = 2 * chip + 1 - core
    other_row = row + 1 - 2 * (row % 2)
    parity = row % 2
    size = block.shape[0]
    own = (pl.ds(pl.multiple_of(parity * third, 16), third))
    others = (pl.ds(pl.multiple_of((1 - parity) * third, 16), third))
    rest = pl.ds(2 * third, size - 2 * third)
    segments = (own, rest)

    barrier = pltpu.get_barrier_semaphore()
    if scatter:
        for k in range(1, n):
            pl.semaphore_signal(barrier, inc=1, device_id={"fsdp": (me + k) % n}, device_id_type=MESH)
        pl.semaphore_signal(barrier, inc=1, device_id={"dp": other_row}, device_id_type=MESH)
        pl.semaphore_wait(barrier, n)
    else:
        for peer in (*neighbour, twin):
            pl.semaphore_signal(barrier, inc=1, device_id={"fsdp": peer}, device_id_type=MESH)
        pl.semaphore_signal(barrier, inc=1, device_id={"dp": other_row}, device_id_type=MESH)
        pl.semaphore_wait(barrier, 4)

    sent = []

    def send(src, dst, send_sem, recv_sem, target):
        copy = pltpu.make_async_remote_copy(
            src_ref=src, dst_ref=dst, send_sem=send_sem, recv_sem=recv_sem,
            device_id=target, device_id_type=MESH,
        )
        copy.start()
        sent.append(copy)

    def arrived(dst, recv_sem, send_sem):
        pltpu.make_async_remote_copy(
            src_ref=dst, dst_ref=dst, send_sem=send_sem, recv_sem=recv_sem,
            device_id={"fsdp": twin}, device_id_type=MESH,
        ).wait_recv()

    hops = ((half, half - 1), (half - 1, half))

    def ring(src, origin, way, seg, step):
        send(
            src, out.at[origin, segments[seg]], ring_send.at[way, seg, step],
            ring_recv.at[way, seg, step], {"fsdp": neighbour[way]},
        )

    for seg in range(2):
        for way in range(2):
            if hops[way][seg] >= 1:
                ring(block.at[segments[seg]], me, way, seg, 0)
    send(block, out.at[me], core_send.at[0, 0, 2], core_recv.at[0, 0, 2], {"fsdp": twin})
    if scatter:
        for k in range(1, n):
            to = (me + k) % n
            send(parts.at[to], mine.at[me], part_send.at[k], part_recv.at[k], {"fsdp": to})
    keep = pltpu.make_async_copy(block, out.at[me], sems.at[0])
    keep.start()
    if scatter:
        keep_part = pltpu.make_async_copy(parts.at[me], mine.at[me], sems.at[1])
        keep_part.start()

    def origin_of(way, step):
        return device_at(place - step if way == 0 else place + step)

    def to_twin(origin, rows, way, step, kind):
        send(
            out.at[origin, rows], out.at[origin, rows], core_send.at[way, step, kind],
            core_recv.at[way, step, kind], {"fsdp": twin},
        )

    def from_row(way, step):
        origin = origin_of(way, step)
        arrived(out.at[origin, others], row_recv.at[way, step], row_send.at[way, step])
        to_twin(origin, others, way, step, 2)

    for step in range(1, half + 1):
        for seg in range(2):
            for way in range(2):
                if step <= hops[way][seg]:
                    origin = origin_of(way, step)
                    rows = segments[seg]
                    view = out.at[origin, rows]
                    arrived(view, ring_recv.at[way, seg, step - 1], ring_send.at[way, seg, step - 1])
                    if step < hops[way][seg]:
                        ring(view, origin, way, seg, step)
                    if seg == 0:
                        send(
                            view, view, row_send.at[way, step], row_recv.at[way, step],
                            {"dp": other_row},
                        )
                    to_twin(origin, rows, way, step, seg)
        for way in range(2):
            if 1 <= step - 1 <= hops[way][0]:
                from_row(way, step - 1)
    for way in range(2):
        if 1 <= half <= hops[way][0]:
            from_row(way, half)

    arrived(out.at[twin], core_recv.at[0, 0, 2], core_send.at[0, 0, 2])
    for way in range(2):
        for step in range(1, half + 1):
            there = origin_of(way, step)
            origin = there + 1 - 2 * core
            for seg in range(2):
                if step <= hops[way][seg]:
                    arrived(
                        out.at[origin, segments[seg]], core_recv.at[way, step, seg],
                        core_send.at[way, step, seg],
                    )
            if step <= hops[way][0]:
                arrived(out.at[origin, others], core_recv.at[way, step, 2], core_send.at[way, step, 2])
    if scatter:
        for k in range(1, n):
            arrived(mine.at[(me + n - k) % n], part_recv.at[k], part_send.at[k])
        keep_part.wait()
    keep.wait()
    for copy in sent:
        copy.wait_send()


def ring_gather(block, collective_id, parts=None):
    n = lax.axis_size("fsdp")
    half = n // 4
    rows, width = block.shape
    third = rows // 16 // 3 * 16
    scatter = parts is not None
    out_shape = [jax.ShapeDtypeStruct((n, rows, width), block.dtype)]
    any_spec = pl.BlockSpec(memory_space=pl.ANY)
    dma = pltpu.SemaphoreType.DMA
    scratch = [
        dma((2,)),
        dma((2, 2, half + 1)), dma((2, 2, half + 1)),
        dma((2, half + 1)), dma((2, half + 1)),
        dma((2, half + 1, 3)), dma((2, half + 1, 3)),
    ]
    operands = [block]
    if scatter:
        out_shape.append(jax.ShapeDtypeStruct(parts.shape, parts.dtype))
        scratch += [dma((n,)), dma((n,))]
        operands.append(parts)
    return pl.pallas_call(
        functools.partial(ring_kernel, scatter, third),
        out_shape=out_shape,
        in_specs=[pl.BlockSpec(memory_space=pltpu.VMEM)] * len(operands),
        out_specs=[any_spec] * len(out_shape),
        scratch_shapes=scratch,
        compiler_params=pltpu.CompilerParams(
            collective_id=collective_id, has_side_effects=True, vmem_limit_bytes=24 * 2**20
        ),
    )(*operands)


def per_device(
    queries,
    keys,
    values,
    lengths,
    normalized_weight,
    block_scale_codes,
    scale_group_factor,
    scale_group_offset,
    adapter_down_weight,
    adapter_up_weight,
    cotangent,
):
    n = lax.axis_size("fsdp")
    row_index = lax.axis_index("dp")
    rank, down_width = adapter_down_weight.shape
    up_width = adapter_up_weight.shape[1]
    own_rows = down_width + up_width
    packed_rows = own_rows * rank // 128
    padded_rows = -(-packed_rows // 16) * 16

    def pack(x):
        x = x.reshape(*x.shape[:-2], packed_rows, 128)
        pad = [(0, 0)] * (x.ndim - 2) + [(0, padded_rows - packed_rows), (0, 0)]
        return jnp.pad(x, pad)

    def unpack(x):
        return x[..., :packed_rows, :].reshape(*x.shape[:-2], own_rows, rank)

    own_lengths = lax.dynamic_index_in_dim(lengths[0], row_index, 0, keepdims=False)
    own_adapters = jnp.concatenate([adapter_up_weight.T, adapter_down_weight.T], axis=0)
    (adapters,) = ring_gather(pack(own_adapters), 0)
    adapters = unpack(adapters)
    up_rows = adapters[:, :up_width].reshape(n * up_width, rank)
    down_rows = adapters[:, up_width:].reshape(n * down_width, rank)

    attention_output = attend(queries, keys, values, own_lengths)
    reduced_activation = jnp.dot(
        attention_output, down_rows, preferred_element_type=jnp.float32
    ).astype(jnp.bfloat16)
    reduced_gradient = (
        adapter_scale * jnp.dot(cotangent, up_rows, preferred_element_type=jnp.float32)
    ).astype(jnp.bfloat16)
    down_part = jnp.dot(attention_output.T, reduced_gradient, preferred_element_type=jnp.float32)
    up_part = adapter_scale * jnp.dot(
        cotangent.T, reduced_activation, preferred_element_type=jnp.float32
    )
    parts = jnp.concatenate(
        [up_part.reshape(n, up_width, rank), down_part.reshape(n, down_width, rank)], axis=1
    ).astype(jnp.bfloat16)

    local_base = dequantize(
        normalized_weight, block_scale_codes, scale_group_factor, scale_group_offset
    )
    gathered, shares = ring_gather(local_base.T, 1, pack(parts))
    base_rows = gathered.reshape(-1, gathered.shape[2])
    share = lax.psum(jnp.sum(shares.astype(jnp.float32), axis=0), "dp")
    share = unpack(share)

    product = lax.dot_general(
        attention_output, base_rows, (((1,), (1,)), ((), ())), preferred_element_type=jnp.float32
    )
    projection_output = (
        product
        + adapter_scale
        * lax.dot_general(
            reduced_activation, up_rows, (((1,), (1,)), ((), ())),
            preferred_element_type=jnp.float32,
        )
    ).astype(jnp.bfloat16)
    attention_gradient = (
        jnp.dot(cotangent, base_rows, preferred_element_type=jnp.float32)
        + lax.dot_general(
            reduced_gradient, down_rows, (((1,), (1,)), ((), ())),
            preferred_element_type=jnp.float32,
        )
    ).astype(jnp.bfloat16)
    return (projection_output, attention_gradient, share[up_width:].T, share[:up_width].T)


def solution(mesh):
    return jax.shard_map(
        per_device,
        mesh=mesh,
        in_specs=(
            P(("dp", "fsdp"), None),
            P(("dp", "fsdp"), None),
            P(("dp", "fsdp"), None),
            P("fsdp", None, None),
            P(None, "fsdp"),
            P(None, "fsdp"),
            P(None, "fsdp"),
            P(None, "fsdp"),
            P(None, "fsdp"),
            P(None, "fsdp"),
            P(("dp", "fsdp"), None),
        ),
        out_specs=(
            P(("dp", "fsdp"), None),
            P(("dp", "fsdp"), None),
            P(None, "fsdp"),
            P(None, "fsdp"),
        ),
        check_vma=False,
    )
```

time: 345 us -> 245 us (0.71)
  waiting for transfers between devices: 210 us -> 0.02 us
  Pallas kernels: 0 us -> 144 us
  blocking collectives: 48 us -> 0 us
  local copies, waits for them, and re-layouts: 22.8 us -> 36.3 us
    pallas_call x0 -> x2, Pallas kernels: none -> 144 us  [ring_gather(): pl.pallas_call(functools.partial(ring_kernel, scatter, third), out_shape=...]
    all_gather x1 -> x0, waiting for transfers between devices: 135 us -> none  [per_device(): lax.all_gather(base_view, 'fsdp', axis=1, tiled=True)]
    unnamed x6 -> x1, waiting for transfers between devices: 74.5 us -> 0.02 us
    all_gather x2 -> x0, blocking collectives: 41 us -> none  [the longest x1 22.9 us: per_device(): lax.all_gather(adapter_down_weight, 'fsdp', axis=1, tiled=True)]
    psum x1 -> x0, blocking collectives: 6.98 us -> none  [per_device(): down_grad, adapter_up_gradient = lax.psum((down_share, up_share), 'dp')]
    slice x0 -> x6, local copies, waits for them, and re-layouts: none -> 5.7 us  [the longest x1 2.45 us: per_device(): down_rows = adapters[:, up_width:].reshape(n * down_width, rank)]
    reshape x0 -> x4, local copies, waits for them, and re-layouts: none -> 4.67 us  [the longest x1 1.79 us: unpack(): return x[..., :packed_rows, :].reshape(*x.shape[:-2], own_rows, rank)]
    convert_element_type x1 -> x0, other arithmetic: 4.03 us -> none  [dequantize(): (normalized_weight.astype(jnp.float32) * jnp.repeat(absmax, QBLOCK, axis=...]
  transfers between devices with their start and end apart: 4 -> 1, of which waited for: 3 -> 0; matrix products, arithmetic and copies ran while one was open for 16% -> 14% of each run, Pallas kernels for 0% -> 0%
where the time goes in v1:
time: 245 us
  Pallas kernels  144 us (59%)
  matrix products  41.7 us (17%)
  local copies, waits for them, and re-layouts  36.3 us (15%)
  between operations  14.2 us (6%)
  other arithmetic  8.63 us (4%)
    pallas_call x2, Pallas kernels, ring_gather(): pl.pallas_call(functools.partial(ring_kernel, scatter, third), out_shape=...  144 us
    dot_general x1, matrix products, per_device(): lax.dot_general(attention_output, base_rows, (((1,), (1,)), ((), ())), pr...  15.2 us
    dot_general x1, matrix products, per_device(): jnp.dot(cotangent, base_rows, preferred_element_type=jnp.float32)  12.5 us
    unnamed x32, local copies, waits for them, and re-layouts  11.9 us
    reshape x1, local copies, waits for them, and re-layouts, dequantize(): jnp.repeat(absmax, QBLOCK, axis=0)  5.3 us
  transfers between devices with their start and end apart: 1, of which 0 were waited for; matrix products, arithmetic and copies ran while one was open for 14% of the time, Pallas kernels for 0%

profile of v1, /device:TPU:11, one launch (start us, length us, event | category | flops | bytes accessed | tf_op | source)
XLA Modules:
  0.0 244.6 jit_solution(5846673494174337739)
XLA Ops:
  7.2 1.0 pad_maximum_fusion.1
  8.5 18.7 %shard_map.138 = bf16[16,240,128]{2,1,0:T(8,128)(2,1)S(1)} custom-call(bf16[240,128]{1,0:T(8,128)(2,1)S(1)} %reshape.134.refs_0_), custom_call_target="tpu_custom_call" | custom-call | tf_op jit(solution)/shard_map/pallas_call | solution.py:219
  27.2 1.8 reshape.135
  29.0 1.4 slice.25
  30.4 2.4 slice.24
  33.3 2.3 fusion.5
  36.7 1.8 fusion.27
  39.5 1.1 copy.92
  40.6 2.4 copy.54
  44.8 1.1 copy.56
  46.0 1.7 convolution_convert_fusion.1
  47.6 1.3 fusion.3
  48.9 1.7 copy.60
  50.6 2.7 %pad_maximum_fusion = bf16[16,480,64]{2,1,0:T(8,128)(2,1)} fusion(bf16[16,160,64]{2,1,0:T(8,128)(2,1)} %copy.56, bf16[16,320,64]{2,1,0:T(8,128)(2,1)S(1)} %bitcast.97), kind=kLoop, calls=%fused_computation.16 | loop fusion | flops 1966080 | bytes 1966080 | tf_op jit(solution)/shard_map/concatenate | solution.py:278
  53.3 2.9 %convert_element_type.47.refs_1_ = bf16[16,240,128]{2,1,0:T(8,128)(2,1)S(1)} reshape(bf16[16,480,64]{2,1,0:T(8,128)(2,1)} %pad_maximum_fusion) | data formatting | bytes 1966080 | tf_op jit(solution)/shard_map/convert_element_type | solution.py:280
  56.3 2.1 broadcast_in_dim.34
  58.5 5.3 %copy.52 = f32[2560,320]{0,1:T(8,128)} copy(f32[2560,320]{1,0:T(8,128)} %bitcast.91) | data formatting | bytes 6553600 | tf_op jit(solution)/shard_map/reshape | solution.py:22
  63.8 2.8 %fusion.15.refs_0_ = bf16[320,2560]{1,0:T(8,128)(2,1)S(1)} fusion(f32[2560,320]{0,1:T(8,128)} %copy.52, bf16[2560,320]{0,1:T(8,128)(2,1)} %param.15), kind=kLoop, calls=%fused_computation.24 | loop fusion | flops 2457600 | bytes 6553600 | tf_op jit(solution)/shard_map/transpose | solution.py:285
  66.6 125.0 %shard_map.139 = (bf16[16,320,2560]{2,1,0:T(8,128)(2,1)S(1)}, bf16[16,240,128]{2,1,0:T(8,128)(2,1)S(1)}) custom-call(bf16[320,2560]{1,0:T(8,128)(2,1)S(1)} %fusion.15.refs_0_, bf16[16,240,128]{2,1,0:T(8,128)(2,1)S(1)} %convert_element_type.47.refs_1_), custom_call_target="tpu_custom_call" | custom-call | tf_op jit(solution)/shard_map/pallas_call | solution.py:219
  191.6 8.6 %copy-done.2 = bf16[16,320,2560]{2,1,0:T(8,128)(2,1)} copy-done((bf16[16,320,2560]{2,1,0:T(8,128)(2,1)}, bf16[16,320,2560]{2,1,0:T(8,128)(2,1)S(1)}, u32[]{:S(2)}) %copy-start.2) | copy-done | bytes 26214424
  201.1 12.5 %convolution_bitcast_fusion = f32[192,2560]{1,0:T(8,128)} fusion(bf16[192,5120]{1,0:T(8,128)(2,1)S(1)} %copy-done, bf16[5120,2560]{1,0:T(8,128)(2,1)} %bitcast.89), kind=kOutput, calls=%fused_computation.9 | convolution fusion | flops 5033164800 | bytes 30146560 | tf_op jit(solution)/shard_map/dot_general | solution.py:302
  213.6 15.2 %fusion.17 = f32[192,5120]{1,0:T(8,128)} fusion(bf16[5120,2560]{1,0:T(8,128)(2,1)} %bitcast.90, bf16[20,24,8,128]{3,2,1,0:T(8,128)(2,1)} %copy-done.8), kind=kOutput, calls=%fused_computation.29 | convolution fusion | flops 5033164800 | bytes 31129600 | tf_op jit(solution)/shard_map/dot_general | solution.py:290
  228.8 4.2 %fusion.1 = bf16[192,5120]{1,0:T(8,128)(2,1)} fusion(f32[192,5120]{1,0:T(8,128)} %fusion.17, bf16[192,64]{0,1:T(8,128)(2,1)S(1)} %convolution_convert_fusion.1, bf16[5120,64]{1,0:T(8,128)(2,1)S(1)} %bitcast.93), kind=kOutput, calls=%fused_computation.2 | convolution fusion | flops 128778240 | bytes 6578176 | tf_op jit(solution)/shard_map/dot_general | solution.py:296
  233.1 1.4 fusion.4
  (49 shorter events, 8.8 us)
Async XLA Ops:
  7.2 35.8 %copy-start = (bf16[192,5120]{1,0:T(8,128)(2,1)S(1)}, bf16[192,5120]{1,0:T(8,128)(2,1)}, u32[]{:S(2)}) copy-start(bf16[192,5120]{1,0:T(8,128)(2,1)} %param.21) | copy-start | bytes 5898244
  7.2 227.3 %all-reduce.2.cloned.1.call-start = ((), (), s32[]{:S(2)}) async-start(), calls=%async_computation | async-start | bytes 245760 | tf_op jit(solution)/shard_map/psum | solution.py:287
  29.0 3.9 %copy-start.14 = (s32[1,2,4]{2,1,0:T(2,128)S(1)}, s32[1,2,4]{2,1,0:T(2,128)}, u32[]{:S(2)}) copy-start(s32[1,2,4]{2,1,0:T(2,128)} %param.14) | copy-start | bytes 100
  30.4 12.5 %copy-start.3 = (bf16[16,320,64]{2,1,0:T(8,128)(2,1)}, bf16[16,320,64]{2,1,0:T(8,128)(2,1)S(1)}, u32[]{:S(2)}) copy-start(bf16[16,320,64]{2,1,0:T(8,128)(2,1)S(1)} %slice.25) | copy-start | bytes 1966084
  35.5 1.2 copy-start.13
  38.5 1.0 copy-start.8
  42.9 1.3 copy-start.7
  43.7 2.2 copy-start.5
  53.3 2.9 %copy-start.10 = (s32[40,320]{1,0:T(8,128)S(1)}, s32[40,320]{1,0:T(8,128)}, u32[]{:S(2)}) copy-start(s32[40,320]{1,0:T(8,128)} %param.16) | copy-start | bytes 153604
  53.3 3.0 %copy-start.11 = (f32[5,320]{1,0:T(8,128)S(1)}, f32[5,320]{1,0:T(8,128)}, u32[]{:S(2)}) copy-start(f32[5,320]{1,0:T(8,128)} %param.18) | copy-start | bytes 19204
  53.3 3.0 %copy-start.12 = (f32[5,320]{1,0:T(8,128)S(1)}, f32[5,320]{1,0:T(8,128)}, u32[]{:S(2)}) copy-start(f32[5,320]{1,0:T(8,128)} %param.17) | copy-start | bytes 19204
  191.6 8.6 %copy-start.2 = (bf16[16,320,2560]{2,1,0:T(8,128)(2,1)}, bf16[16,320,2560]{2,1,0:T(8,128)(2,1)S(1)}, u32[]{:S(2)}) copy-start(bf16[16,320,2560]{2,1,0:T(8,128)(2,1)S(1)} %get-tuple-element.6) | copy-start | bytes 78643200
  213.6 15.2 %copy-start.4 = (bf16[16,320,64]{2,1,0:T(8,128)(2,1)S(1)}, bf16[16,320,64]{2,1,0:T(8,128)(2,1)}, u32[]{:S(2)}) copy-start(bf16[16,320,64]{2,1,0:T(8,128)(2,1)} %copy-done.3) | copy-start | bytes 1966084
  228.8 4.3 %copy-start.6 = (bf16[16,160,64]{2,1,0:T(8,128)(2,1)S(1)}, bf16[16,160,64]{2,1,0:T(8,128)(2,1)}, u32[]{:S(2)}) copy-start(bf16[16,160,64]{2,1,0:T(8,128)(2,1)} %slice.24) | copy-start | bytes 983044
  228.8 4.3 %copy-start.9 = (f32[192,2560]{1,0:T(8,128)S(1)}, f32[192,2560]{1,0:T(8,128)}, u32[]{:S(2)}) copy-start(f32[192,2560]{1,0:T(8,128)} %convolution_bitcast_fusion) | copy-start | bytes 5898244
  228.8 9.0 %copy-start.1 = (bf16[192,5120]{1,0:T(8,128)(2,1)S(1)}, bf16[192,5120]{1,0:T(8,128)(2,1)}, u32[]{:S(2)}) copy-start(bf16[192,5120]{1,0:T(8,128)(2,1)} %param.21) | copy-start | bytes 5898244
Sparse Core Ops, SparseCore 0:
  201.2 18.6 all-reduce.1

commit v2 on v1

--- a/solution.py
+++ b/solution.py
@@ -15,13 +15,27 @@
 adapter_scale = 0.25
 
 
+def dequantize_kernel(weight, absmax, out):
+    rows, features = out.shape
+    lane = lax.broadcasted_iota(jnp.int32, (rows, 2 * QBLOCK), 1)
+    for i in range(features // (2 * QBLOCK)):
+        columns = slice(2 * QBLOCK * i, 2 * QBLOCK * (i + 1))
+        scale = jnp.where(
+            lane < QBLOCK, absmax[:, 2 * i : 2 * i + 1], absmax[:, 2 * i + 1 : 2 * i + 2]
+        )
+        out[:, columns] = (weight[:, columns].astype(jnp.float32) * scale).astype(out.dtype)
+
+
 def dequantize(normalized_weight, block_scale_codes, scale_group_factor, scale_group_offset):
     spread_scale = jnp.repeat(scale_group_factor, SCALE_GROUP, axis=0)
     spread_offset = jnp.repeat(scale_group_offset, SCALE_GROUP, axis=0)
     absmax = spread_scale * (block_scale_codes.astype(jnp.float32) + 1.0) / 256.0 + spread_offset
-    return (normalized_weight.astype(jnp.float32) * jnp.repeat(absmax, QBLOCK, axis=0)).astype(
-        jnp.bfloat16
-    )
+    weight = normalized_weight.T
+    return pl.pallas_call(
+        dequantize_kernel,
+        out_shape=jax.ShapeDtypeStruct(weight.shape, jnp.bfloat16),
+        compiler_params=pltpu.CompilerParams(vmem_limit_bytes=16 * 2**20),
+    )(weight, absmax.T)
 
 
 def attend(queries, keys, values, doc_lengths):
@@ -200,7 +214,7 @@
     n = lax.axis_size("fsdp")
     half = n // 4
     rows, width = block.shape
-    third = rows // 16 // 3 * 16
+    third = (rows // 16 + 2) // 3 * 16
     scatter = parts is not None
     out_shape = [jax.ShapeDtypeStruct((n, rows, width), block.dtype)]
     any_spec = pl.BlockSpec(memory_space=pl.ANY)
@@ -226,6 +240,55 @@
             collective_id=collective_id, has_side_effects=True, vmem_limit_bytes=24 * 2**20
         ),
     )(*operands)
+
+
+def row_sum_kernel(rows, share, out, landed, send_sems, recv_sems):
+    me = lax.axis_index("dp")
+    barrier = pltpu.get_barrier_semaphore()
+    for k in range(1, rows):
+        pl.semaphore_signal(barrier, inc=1, device_id={"dp": (me + k) % rows}, device_id_type=MESH)
+    pl.semaphore_wait(barrier, rows - 1)
+    copies = []
+    for k in range(1, rows):
+        copy = pltpu.make_async_remote_copy(
+            src_ref=share, dst_ref=landed.at[me], send_sem=send_sems.at[k],
+            recv_sem=recv_sems.at[k], device_id={"dp": (me + k) % rows}, device_id_type=MESH,
+        )
+        copy.start()
+        copies.append(copy)
+    keep = pltpu.make_async_copy(share, landed.at[me], send_sems.at[0])
+    keep.start()
+    for k in range(1, rows):
+        pltpu.make_async_remote_copy(
+            src_ref=share, dst_ref=landed.at[(me + rows - k) % rows], send_sem=send_sems.at[k],
+            recv_sem=recv_sems.at[k], device_id={"dp": (me + k) % rows}, device_id_type=MESH,
+        ).wait_recv()
+    keep.wait()
+    for copy in copies:
+        copy.wait_send()
+    total = landed[0]
+    for k in range(1, rows):
+        total = total + landed[k]
+    out[...] = total
+
+
+def sum_over_rows(share):
+    rows = lax.axis_size("dp")
+    vmem = pl.BlockSpec(memory_space=pltpu.VMEM)
+    return pl.pallas_call(
+        functools.partial(row_sum_kernel, rows),
+        out_shape=jax.ShapeDtypeStruct(share.shape, share.dtype),
+        in_specs=[vmem],
+        out_specs=vmem,
+        scratch_shapes=[
+            pltpu.VMEM((rows, *share.shape), share.dtype),
+            pltpu.SemaphoreType.DMA((rows,)),
+            pltpu.SemaphoreType.DMA((rows,)),
+        ],
+        compiler_params=pltpu.CompilerParams(
+            collective_id=2, has_side_effects=True, vmem_limit_bytes=16 * 2**20
+        ),
+    )(share)
 
 
 def per_device(
@@ -282,10 +345,9 @@
     local_base = dequantize(
         normalized_weight, block_scale_codes, scale_group_factor, scale_group_offset
     )
-    gathered, shares = ring_gather(local_base.T, 1, pack(parts))
+    gathered, shares = ring_gather(local_base, 1, pack(parts))
     base_rows = gathered.reshape(-1, gathered.shape[2])
-    share = lax.psum(jnp.sum(shares.astype(jnp.float32), axis=0), "dp")
-    share = unpack(share)
+    share = unpack(sum_over_rows(jnp.sum(shares.astype(jnp.float32), axis=0)))
 
     product = lax.dot_general(
         attention_output, base_rows, (((1,), (1,)), ((), ())), preferred_element_type=jnp.float32

time: 245 us -> 228 us (0.931)
  between operations: 14.2 us -> 0.94 us
  Pallas kernels: 144 us -> 152 us
  local copies, waits for them, and re-layouts: 36.3 us -> 30.4 us
  other arithmetic: 8.63 us -> 4.24 us
  matrix products: 41.7 us -> 39.1 us
    pallas_call x0 -> x2, Pallas kernels: none -> 6.78 us  [the longest x1 4.97 us: sum_over_rows(): pl.pallas_call(functools.partial(row_sum_kernel, rows), out_shape=jax.Sha...]
    unnamed x32 -> x38, local copies, waits for them, and re-layouts: 11.9 us -> 15.7 us
    reshape x1 -> x4, local copies, waits for them, and re-layouts: 5.3 us -> 1.67 us  [the longest x2 1.56 us: dequantize(): spread_offset = jnp.repeat(scale_group_offset, SCALE_GROUP, axis=0)]
    transpose x1, other arithmetic: 2.82 us -> 0.03 us  [dequantize(): return pl.pallas_call(dequantize_kernel, out_shape=jax.ShapeDtypeStruct(w...]
  transfers between devices with their start and end apart: 1 -> 0, of which waited for: 0 -> 0; matrix products, arithmetic and copies ran while one was open for 14% -> 0% of each run, Pallas kernels for 0% -> 0%
where the time goes in v2:
time: 228 us; the launch traced here: 227 us
  Pallas kernels  152 us (67%)
  matrix products  39.1 us (17%)
  local copies, waits for them, and re-layouts  30.4 us (13%)
  other arithmetic  4.24 us (2%)
    pallas_call x2, Pallas kernels, ring_gather(): pl.pallas_call(functools.partial(ring_kernel, scatter, third), out_shape=...  146 us
    unnamed x38, local copies, waits for them, and re-layouts  15.7 us
    dot_general x1, matrix products, per_device(): lax.dot_general(attention_output, base_rows, (((1,), (1,)), ((), ())), pr...  15.1 us
    dot_general x1, matrix products, per_device(): jnp.dot(cotangent, base_rows, preferred_element_type=jnp.float32)  11.2 us
    pallas_call x1, Pallas kernels, sum_over_rows(): pl.pallas_call(functools.partial(row_sum_kernel, rows), out_shape=jax.Sha...  4.97 us

profile of v2, /device:TPU:11, one launch (start us, length us, event | category | flops | bytes accessed | tf_op | source)
XLA Modules:
  0.0 227.0 jit_solution(7991489578499428894)
XLA Ops:
  1.8 2.3 fusion.5
  5.3 1.8 fusion.26
  7.1 1.0 copy-done.10
  8.3 1.4 copy.78
  10.0 18.7 %shard_map.139 = bf16[16,240,128]{2,1,0:T(8,128)(2,1)S(1)} custom-call(bf16[240,128]{1,0:T(8,128)(2,1)S(1)} %reshape.130.refs_0_), custom_call_target="tpu_custom_call" | custom-call | tf_op jit(solution)/shard_map/pallas_call | solution.py:233
  28.7 1.8 reshape.131
  30.5 1.4 slice.25
  31.9 1.0 copy-done.5
  34.3 1.1 copy.80
  35.5 1.1 slice.24
  37.9 1.3 fusion.3
  39.2 1.7 copy.84
  40.9 2.7 %pad_maximum_fusion = bf16[16,480,64]{2,1,0:T(8,128)(2,1)} fusion(bf16[16,160,64]{2,1,0:T(8,128)(2,1)} %copy.80, bf16[16,320,64]{2,1,0:T(8,128)(2,1)S(1)} %bitcast.93), kind=kLoop, calls=%fused_computation.15 | loop fusion | flops 1966080 | bytes 1966080 | tf_op jit(solution)/shard_map/concatenate | solution.py:341
  43.7 2.9 %convert_element_type.39.refs_1_ = bf16[16,240,128]{2,1,0:T(8,128)(2,1)S(1)} reshape(bf16[16,480,64]{2,1,0:T(8,128)(2,1)} %pad_maximum_fusion) | data formatting | bytes 1966080 | tf_op jit(solution)/shard_map/convert_element_type | solution.py:343
  48.5 1.4 copy-done.1
  49.9 1.8 shard_map.138.refs_0_
  51.7 126.9 %shard_map.140 = (bf16[16,320,2560]{2,1,0:T(8,128)(2,1)S(1)}, bf16[16,240,128]{2,1,0:T(8,128)(2,1)S(1)}) custom-call(bf16[320,2560]{1,0:T(8,128)(2,1)S(1)} %shard_map.138.refs_0_, bf16[16,240,128]{2,1,0:T(8,128)(2,1)S(1)} %convert_element_type.39.refs_1_), custom_call_target="tpu_custom_call" | custom-call | tf_op jit(solution)/shard_map/pallas_call | solution.py:233
  178.6 1.0 copy-done.2
  179.6 8.6 %copy-done.4 = bf16[16,320,2560]{2,1,0:T(8,128)(2,1)} copy-done((bf16[16,320,2560]{2,1,0:T(8,128)(2,1)}, bf16[16,320,2560]{2,1,0:T(8,128)(2,1)S(1)}, u32[]{:S(2)}) %copy-start.4) | copy-done | bytes 26214424
  188.3 11.2 %convolution_bitcast_fusion = f32[192,2560]{1,0:T(8,128)S(1)} fusion(bf16[192,5120]{1,0:T(8,128)(2,1)S(1)} %copy-done, bf16[5120,2560]{1,0:T(8,128)(2,1)} %bitcast.86), kind=kOutput, calls=%fused_computation.9 | convolution fusion | flops 5033164800 | bytes 30146560 | tf_op jit(solution)/shard_map/dot_general | solution.py:364
  199.5 1.4 fusion.4
  200.9 15.1 %fusion.16 = f32[192,5120]{1,0:T(8,128)} fusion(bf16[5120,2560]{1,0:T(8,128)(2,1)} %bitcast.87, bf16[20,24,8,128]{3,2,1,0:T(8,128)(2,1)} %copy-done.10), kind=kOutput, calls=%fused_computation.27 | convolution fusion | flops 5033164800 | bytes 31129600 | tf_op jit(solution)/shard_map/dot_general | solution.py:352
  216.0 4.2 %fusion.1 = bf16[192,5120]{1,0:T(8,128)(2,1)} fusion(f32[192,5120]{1,0:T(8,128)} %fusion.16, bf16[192,64]{0,1:T(8,128)(2,1)S(1)} %convolution_convert_fusion.1, bf16[5120,64]{1,0:T(8,128)(2,1)S(1)} %bitcast.89), kind=kOutput, calls=%fused_computation.2 | convolution fusion | flops 128778240 | bytes 6578176 | tf_op jit(solution)/shard_map/dot_general | solution.py:358
  220.4 5.0 %shard_map.141 = f32[240,128]{1,0:T(8,128)S(1)} custom-call(f32[240,128]{1,0:T(8,128)S(1)} %convert_reduce_fusion.share), custom_call_target="tpu_custom_call" | custom-call | tf_op jit(solution)/shard_map/pallas_call | solution.py:278
  (57 shorter events, 9.2 us)
Async XLA Ops:
  0.6 32.3 %copy-start = (bf16[192,5120]{1,0:T(8,128)(2,1)S(1)}, bf16[192,5120]{1,0:T(8,128)(2,1)}, u32[]{:S(2)}) copy-start(bf16[192,5120]{1,0:T(8,128)(2,1)} %param.21) | copy-start | bytes 5898244
  4.1 1.2 copy-start.17
  7.1 1.0 copy-start.10
  8.1 1.6 copy-start.13
  8.1 1.6 copy-start.14
  31.9 1.1 copy-start.5
  31.9 1.9 copy-start.9
  33.8 3.7 %copy-start.11 = (bf16[20,24,8,128]{3,2,1,0:T(8,128)(2,1)S(1)}, bf16[20,24,8,128]{3,2,1,0:T(8,128)(2,1)}, u32[]{:S(2)}) copy-start(bf16[20,24,8,128]{3,2,1,0:T(8,128)(2,1)} %copy-done.10) | copy-start | bytes 2949124
  36.6 0.8 copy-start.7
  43.6 2.9 %copy-start.12 = (s32[40,320]{1,0:T(8,128)S(1)}, s32[40,320]{1,0:T(8,128)}, u32[]{:S(2)}) copy-start(s32[40,320]{1,0:T(8,128)} %param.16) | copy-start | bytes 153604
  43.7 3.1 %copy-start.15 = (f32[5,320]{1,0:T(8,128)S(1)}, f32[5,320]{1,0:T(8,128)}, u32[]{:S(2)}) copy-start(f32[5,320]{1,0:T(8,128)} %param.17) | copy-start | bytes 19204
  43.7 3.2 %copy-start.16 = (f32[5,320]{1,0:T(8,128)S(1)}, f32[5,320]{1,0:T(8,128)}, u32[]{:S(2)}) copy-start(f32[5,320]{1,0:T(8,128)} %param.18) | copy-start | bytes 19204
  48.5 1.4 copy-start.1
  178.6 1.0 copy-start.2
  179.6 8.6 %copy-start.4 = (bf16[16,320,2560]{2,1,0:T(8,128)(2,1)}, bf16[16,320,2560]{2,1,0:T(8,128)(2,1)S(1)}, u32[]{:S(2)}) copy-start(bf16[16,320,2560]{2,1,0:T(8,128)(2,1)S(1)} %get-tuple-element.6) | copy-start | bytes 78643200
  188.3 11.3 %copy-start.8 = (bf16[16,160,64]{2,1,0:T(8,128)(2,1)S(1)}, bf16[16,160,64]{2,1,0:T(8,128)(2,1)}, u32[]{:S(2)}) copy-start(bf16[16,160,64]{2,1,0:T(8,128)(2,1)} %copy-done.7) | copy-start | bytes 983044
  200.9 15.1 %copy-start.6 = (bf16[16,320,64]{2,1,0:T(8,128)(2,1)S(1)}, bf16[16,320,64]{2,1,0:T(8,128)(2,1)}, u32[]{:S(2)}) copy-start(bf16[16,320,64]{2,1,0:T(8,128)(2,1)} %copy-done.5) | copy-start | bytes 1966084
  216.0 4.2 %copy-start.3 = (bf16[16,240,128]{2,1,0:T(8,128)(2,1)S(1)}, bf16[16,240,128]{2,1,0:T(8,128)(2,1)}, u32[]{:S(2)}) copy-start(bf16[16,240,128]{2,1,0:T(8,128)(2,1)} %copy-done.2) | copy-start | bytes 2949124
